TPU v7x, 256 devices: a whole 4x4x8 slice. The times are simulated.
256 devices in a mesh: tm: 64 (over z, x, core), blk: 4 (over y).
Axes of the slice: x: 4, y: 4, z: 8, core: 2. Of those that a mesh axis runs over, the one named last changes fastest.
Arguments:
- prior_mean: float32 [512], replicated, may hold values from -6 to 6
- after_mean: float32 [512], replicated, may hold values from -6 to 6
- filter_map: float32 [128, 512, 512], P('tm', 'blk'), may hold values from -1 to 1.5
- smoother_gain: float32 [128, 512, 512], P('tm', 'blk'), may hold values from -1 to 1.5
- smoother_map: float32 [128, 512, 512], P('tm', 'blk'), may hold values from -1 to 1.5
- obs_gain: float32 [128, 512, 128], P('tm', 'blk'), may hold values from -0.5 to 0.5
- observations: float32 [128, 128], P('tm'), may hold values from -6 to 6
Outputs:
- filtered: float32 [128, 512], P('tm', 'blk')
- smoothed: float32 [128, 512], P('tm', 'blk')
All inputs are finite; a program needn't handle non-finite values.
Results may differ from a plain program's by a relative error of at most 0.0003.
Values sent between devices are 32-bit elements; how exact they have to be, the bound alone decides.
A program may use at most 128 MiB of HBM per device.

v0:
```python
import jax
import jax.numpy as jnp
from jax import lax
from jax.sharding import Mesh
from jax.sharding import PartitionSpec as P

TM = ("tm_0", "tm_1", "tm_2")


def neutral_like(value, identity):
    return jax.tree.map(
        lambda part, zero: jnp.zeros_like(part) + jnp.asarray(zero, part.dtype), value, identity
    )


def prefix_by_axis(value, axes, combine, identity, reverse):
    before = start = neutral_like(value, identity)
    so_far = value
    for axis in reversed(axes):
        length, index = (lax.axis_size(axis), lax.axis_index(axis))
        pieces = jax.tree.map(lambda part: lax.all_gather(part, axis), so_far)
        inside, so_far = (start, start)
        for k in reversed(range(length)) if reverse else range(length):
            passed = k > index if reverse else k < index
            so_far = combine(so_far, jax.tree.map(lambda part: part[k], pieces))
            inside = jax.tree.map(lambda new, old: jnp.where(passed, new, old), so_far, inside)
        before = combine(inside, before)
    return before


def chain_combine(earlier, later):
    highest = lax.Precision.HIGHEST
    joined_map = jnp.dot(later[0], earlier[0], precision=highest)
    joined_offset = jnp.dot(later[0], earlier[1], precision=highest) + later[1]
    return (joined_map, joined_offset)


def shards(prior_mean, after_mean, filter_map, smoother_gain, smoother_map, obs_gain, observations):
    highest = lax.Precision.HIGHEST
    steps = filter_map.shape[0]
    rows = filter_map.shape[1]
    width = filter_map.shape[2]
    first_row = lax.axis_index("blk") * rows
    drive_rows = jnp.einsum("tro,to->tr", obs_gain, observations, precision=highest)
    full_filter, full_gain, drive = (
        lax.all_gather(filter_map, "blk", axis=1, tiled=True),
        lax.all_gather(smoother_gain, "blk", axis=1, tiled=True),
        lax.all_gather(drive_rows, "blk", axis=1, tiled=True),
    )
    identity = jnp.eye(width, dtype=jnp.float32)
    nothing = jnp.zeros((width,), jnp.float32)
    offset = nothing
    for index in range(steps):
        offset = jnp.dot(full_filter[index], offset, precision=highest) + drive[index]
    composite = full_filter[steps - 1]
    index = 0
    composite = jnp.dot(composite, full_filter[index], precision=highest)
    total = prefix_by_axis((composite, offset), TM, chain_combine, (identity, nothing), False)
    entering = jnp.dot(total[0], prior_mean, precision=highest) + total[1]
    current = entering
    filtered_list = []
    for index in range(steps):
        current = jnp.dot(full_filter[index], current, precision=highest) + drive[index]
        filtered_list.append(current)
    filtered_full = jnp.stack(filtered_list, axis=0)
    filtered_rows = lax.dynamic_slice_in_dim(filtered_full, first_row, rows, 1)
    pulled_rows = jnp.einsum("trk,tk->tr", smoother_map, filtered_full, precision=highest)
    pulled = lax.all_gather(pulled_rows, "blk", axis=1, tiled=True)
    offset = nothing
    for index in range(steps - 1, -1, -1):
        offset = jnp.dot(full_gain[index], offset, precision=highest) + pulled[index]
    composite = full_gain[0]
    index = 1
    composite = jnp.dot(composite, full_gain[index], precision=highest)
    total = prefix_by_axis((composite, offset), TM, chain_combine, (identity, nothing), True)
    leaving = jnp.dot(total[0], after_mean, precision=highest) + total[1]
    current = leaving
    smoothed_list = []
    for index in range(steps - 1, -1, -1):
        current = jnp.dot(full_gain[index], current, precision=highest) + pulled[index]
        smoothed_list.append(current)
    smoothed_full = jnp.stack(smoothed_list[::-1], axis=0)
    smoothed_rows = lax.dynamic_slice_in_dim(smoothed_full, first_row, rows, 1)
    return (filtered_rows, smoothed_rows)


def solution(mesh):
    torus = Mesh(mesh.devices.reshape(8, 4, 2, mesh.shape["blk"]), ("tm_0", "tm_1", "tm_2", "blk"))
    in_specs = (
        P(),
        P(),
        P(TM, "blk", None),
        P(TM, "blk", None),
        P(TM, "blk", None),
        P(TM, "blk", None),
        P(TM, None),
    )
    out_specs = (P(TM, "blk"), P(TM, "blk"))
    return jax.shard_map(
        shards, mesh=torus, in_specs=in_specs, out_specs=out_specs, check_vma=False
    )
```

profile of v0, /device:TPU:1, one launch (start us, length us, event | category | flops | bytes accessed | tf_op | source)
XLA Modules:
  0.0 462.8 jit_solution(7283257458123513231)
XLA Ops:
  8.7 38.1 %all-gather.27.cloned.1.call-done = f32[2,512,512]{2,1,0:T(8,128)} async-done(((f32[2,128,512]{2,1,0:T(8,128)}), f32[2,512,512]{2,1,0:T(8,128)}) %all-gather.27.cloned.1.call-update) | async-done | bytes 2097168 | tf_op jit(solution)/shard_map/all_gather | solution.py:46
  46.8 4.4 fusion.142
  51.2 30.8 %all-gather.29.cloned.1.call-done = f32[2,512,512]{2,1,0:T(8,128)} async-done(((f32[2,128,512]{2,1,0:T(8,128)}), f32[2,512,512]{2,1,0:T(8,128)}) %all-gather.29.cloned.1.call-update) | async-done | bytes 2097168 | tf_op jit(solution)/shard_map/all_gather | solution.py:47
  82.0 4.4 fusion.147
  86.5 14.2 %all-gather.31.cloned.1.call-done = f32[1024,512]{1,0:T(8,128)} async-done(((f32[512,512]{1,0:T(8,128)}), f32[1024,512]{1,0:T(8,128)}) %all-gather.31.cloned.1.call-update) | async-done | bytes 2097168 | tf_op jit(solution)/shard_map/all_gather | solution.py:21
  102.9 4.4 fusion.136
  107.4 12.2 %all-gather.37.cloned.1.call-done = f32[1024,512]{1,0:T(8,128)} async-done(((f32[512,512]{1,0:T(8,128)}), f32[1024,512]{1,0:T(8,128)}) %all-gather.37.cloned.1.call-update) | async-done | bytes 2097168 | tf_op jit(solution)/shard_map/all_gather | solution.py:21
  121.8 4.4 fusion.84
  126.7 45.7 %all-gather.33.cloned.1.call-done = f32[2048,512]{1,0:T(8,128)} async-done(((f32[512,512]{1,0:T(8,128)}), f32[2048,512]{1,0:T(8,128)}) %all-gather.33.cloned.1.call-update) | async-done | bytes 4194320 | tf_op jit(solution)/shard_map/all_gather | solution.py:21
  175.8 3.1 fusion.121
  182.7 2.8 fusion.129
  186.0 8.1 %all_gather.91 = f32[2,512]{1,0:T(2,128)S(1)} all-gather(f32[2,128]{1,0:T(2,128)S(1)} %bitcast.347), channel_id=1, replica_groups=mesh['tm_0'=8,'tm_1'=4,'tm_2'=2,'blk'=4] {'blk'}, dimensions={1}, use_global_device_ids=true | all-gather | bytes 5120 | tf_op jit(solution)/shard_map/all_gather | solution.py:48
  198.5 4.2 all-gather.12
  203.6 21.6 %all-gather.39.cloned.1.call-done = f32[2048,512]{1,0:T(8,128)} async-done(((f32[512,512]{1,0:T(8,128)}), f32[2048,512]{1,0:T(8,128)}) %all-gather.39.cloned.1.call-update) | async-done | bytes 4194320 | tf_op jit(solution)/shard_map/all_gather | solution.py:21
  228.5 3.1 fusion.69
  235.5 2.8 fusion.77
  238.4 2.5 fusion.134
  243.2 9.4 %all-gather.13 = f32[4,1,512]{2,1,0:T(1,128)S(1)} all-gather(f32[1,1,512]{2,1,0:T(1,128)S(1)} %bitcast.331), channel_id=6, replica_groups=mesh['tm_0'=8,'tm_1'=4,'tm_2'=2,'blk'=4] {'tm_1'}, dimensions={0}, use_global_device_ids=true | all-gather | bytes 10240 | tf_op jit(solution)/shard_map/all_gather | solution.py:21
  261.6 22.3 %all-gather.14 = f32[8,1,512]{2,1,0:T(1,128)S(1)} all-gather(f32[1,1,512]{2,1,0:T(1,128)S(1)} %bitcast.342), channel_id=7, replica_groups=mesh['tm_0'=8,'tm_1'=4,'tm_2'=2,'blk'=4] {'tm_0'}, dimensions={0}, use_global_device_ids=true | all-gather | bytes 18432 | tf_op jit(solution)/shard_map/all_gather | solution.py:21
  283.9 2.4 fusion.67
  287.3 3.0 fusion.6
  290.3 3.0 fusion.20
  293.3 28.5 %all-gather.35.cloned.1.call-done = f32[4096,512]{1,0:T(8,128)} async-done(((f32[512,512]{1,0:T(8,128)}), f32[4096,512]{1,0:T(8,128)}) %all-gather.35.cloned.1.call-update) | async-done | bytes 8388624 | tf_op jit(solution)/shard_map/all_gather | solution.py:21
  324.1 2.3 fusion.93
  326.5 2.5 fusion.97
  361.3 8.5 %all_gather.105 = f32[2,512]{1,0:T(2,128)S(1)} all-gather(f32[2,128]{1,0:T(2,128)S(1)} %bitcast.346), channel_id=1, replica_groups=mesh['tm_0'=8,'tm_1'=4,'tm_2'=2,'blk'=4] {'blk'}, dimensions={1}, use_global_device_ids=true | all-gather | bytes 5120 | tf_op jit(solution)/shard_map/all_gather | solution.py:68
  370.8 3.6 all-gather.15
  375.4 9.5 %all-gather.16 = f32[4,1,512]{2,1,0:T(1,128)S(1)} all-gather(f32[1,1,512]{2,1,0:T(1,128)S(1)} %bitcast.330), channel_id=12, replica_groups=mesh['tm_0'=8,'tm_1'=4,'tm_2'=2,'blk'=4] {'tm_1'}, dimensions={0}, use_global_device_ids=true | all-gather | bytes 10240 | tf_op jit(solution)/shard_map/all_gather | solution.py:21
  387.9 19.5 %all-gather.17 = f32[8,1,512]{2,1,0:T(1,128)S(1)} all-gather(f32[1,1,512]{2,1,0:T(1,128)S(1)} %bitcast.339), channel_id=13, replica_groups=mesh['tm_0'=8,'tm_1'=4,'tm_2'=2,'blk'=4] {'tm_0'}, dimensions={0}, use_global_device_ids=true | all-gather | bytes 18432 | tf_op jit(solution)/shard_map/all_gather | solution.py:21
  408.7 7.8 %all-gather.41.cloned.1.call-done = f32[4096,512]{1,0:T(8,128)} async-done(((f32[512,512]{1,0:T(8,128)}), f32[4096,512]{1,0:T(8,128)}) %all-gather.41.cloned.1.call-update) | async-done | bytes 8388624 | tf_op jit(solution)/shard_map/all_gather | solution.py:21
  418.8 2.3 fusion.41
  421.2 2.5 fusion.45
  (206 shorter events, 114.0 us)
Async XLA Ops:
  7.2 353.7 %copy-start = (f32[2,128,512]{2,1,0:T(8,128)S(1)}, f32[2,128,512]{2,1,0:T(8,128)}, u32[]{:S(2)}) copy-start(f32[2,128,512]{2,1,0:T(8,128)} %param.11) | copy-start | bytes 1572868
  7.2 39.6 %all-gather.27.cloned.1.call-start = ((), (), s32[]{:S(2)}) async-start(), calls=%async_computation | async-start | bytes 2621440 | tf_op jit(solution)/shard_map/all_gather | solution.py:46
  7.9 74.1 %all-gather.29.cloned.1.call-start = ((), (), s32[]{:S(2)}) async-start(), calls=%async_computation.1 | async-start | bytes 2621440 | tf_op jit(solution)/shard_map/all_gather | solution.py:47
  8.7 92.0 %all-gather.31.cloned.1.call-start = ((), (), s32[]{:S(2)}) async-start(), calls=%async_computation.2 | async-start | bytes 3145728 | tf_op jit(solution)/shard_map/all_gather | solution.py:21
  51.2 68.4 %all-gather.37.cloned.1.call-start = ((), (), s32[]{:S(2)}) async-start(), calls=%async_computation.5 | async-start | bytes 3145728 | tf_op jit(solution)/shard_map/all_gather | solution.py:21
  86.4 86.0 %all-gather.33.cloned.1.call-start = ((), (), s32[]{:S(2)}) async-start(), calls=%async_computation.3 | async-start | bytes 5242880 | tf_op jit(solution)/shard_map/all_gather | solution.py:21
  102.9 23.3 %copy-start.13 = (f32[512,512]{1,0:T(8,128)}, f32[512,512]{1,0:T(8,128)S(1)}, u32[]{:S(2)}) copy-start(f32[512,512]{1,0:T(8,128)S(1)} %fusion.35) | copy-start | bytes 3145732
  107.3 117.9 %all-gather.39.cloned.1.call-start = ((), (), s32[]{:S(2)}) async-start(), calls=%async_computation.6 | async-start | bytes 5242880 | tf_op jit(solution)/shard_map/all_gather | solution.py:21
  121.8 53.0 %copy-start.16 = (f32[512,512]{1,0:T(8,128)}, f32[512,512]{1,0:T(8,128)S(1)}, u32[]{:S(2)}) copy-start(f32[512,512]{1,0:T(8,128)S(1)} %fusion.31) | copy-start | bytes 3145732
  126.2 195.6 %all-gather.35.cloned.1.call-start = ((), (), s32[]{:S(2)}) async-start(), calls=%async_computation.4 | async-start | bytes 9437184 | tf_op jit(solution)/shard_map/all_gather | solution.py:21
  172.4 7.4 %copy-start.7 = (f32[2048,512]{1,0:T(8,128)S(1)}, f32[2048,512]{1,0:T(8,128)}, u32[]{:S(2)}) copy-start(f32[2048,512]{1,0:T(8,128)} %all-gather.33.cloned.1.call-done) | copy-start | bytes 12582916
  179.8 22.8 %copy-start.3 = (f32[2,512,512]{2,1,0:T(8,128)S(1)}, f32[2,512,512]{2,1,0:T(8,128)}, u32[]{:S(2)}) copy-start(f32[2,512,512]{2,1,0:T(8,128)} %all-gather.29.cloned.1.call-done) | copy-start | bytes 6291460
  185.6 231.0 %all-gather.41.cloned.1.call-start = ((), (), s32[]{:S(2)}) async-start(), calls=%async_computation.7 | async-start | bytes 9437184 | tf_op jit(solution)/shard_map/all_gather | solution.py:21
  225.2 7.4 %copy-start.5 = (f32[2048,512]{1,0:T(8,128)S(1)}, f32[2048,512]{1,0:T(8,128)}, u32[]{:S(2)}) copy-start(f32[2048,512]{1,0:T(8,128)} %all-gather.39.cloned.1.call-done) | copy-start | bytes 12582916
  238.3 16.8 %copy-start.14 = (f32[512,512]{1,0:T(8,128)S(1)}, f32[512,512]{1,0:T(8,128)}, u32[]{:S(2)}) copy-start(f32[512,512]{1,0:T(8,128)} %copy-done.13) | copy-start | bytes 3145732
  238.3 16.8 %copy-start.15 = (f32[512,512]{1,0:T(8,128)S(1)}, f32[512,512]{1,0:T(8,128)}, u32[]{:S(2)}) copy-start(f32[512,512]{1,0:T(8,128)} %fusion.136) | copy-start | bytes 3145732
  238.3 18.0 %copy-start.17 = (f32[512,512]{1,0:T(8,128)S(1)}, f32[512,512]{1,0:T(8,128)}, u32[]{:S(2)}) copy-start(f32[512,512]{1,0:T(8,128)} %copy-done.16) | copy-start | bytes 3145732
  238.3 18.0 %copy-start.18 = (f32[512,512]{1,0:T(8,128)S(1)}, f32[512,512]{1,0:T(8,128)}, u32[]{:S(2)}) copy-start(f32[512,512]{1,0:T(8,128)} %fusion.84) | copy-start | bytes 3145732
  240.8 16.8 %copy-start.8 = (f32[2048,512]{1,0:T(8,128)S(1)}, f32[2048,512]{1,0:T(8,128)}, u32[]{:S(2)}) copy-start(f32[2048,512]{1,0:T(8,128)} %all-gather.33.cloned.1.call-done) | copy-start | bytes 12582916
  256.4 30.9 %copy-start.10 = (f32[512,512]{1,0:T(8,128)S(1)}, f32[512,512]{1,0:T(8,128)}, u32[]{:S(2)}) copy-start(f32[512,512]{1,0:T(8,128)} %copy-done.9) | copy-start | bytes 3145732
  256.4 30.9 %copy-start.12 = (f32[512,512]{1,0:T(8,128)S(1)}, f32[512,512]{1,0:T(8,128)}, u32[]{:S(2)}) copy-start(f32[512,512]{1,0:T(8,128)} %copy-done.11) | copy-start | bytes 3145732
  256.4 30.9 %copy-start.25 = (f32[512,512]{1,0:T(8,128)S(1)}, f32[512,512]{1,0:T(8,128)}, u32[]{:S(2)}) copy-start(f32[512,512]{1,0:T(8,128)} %fusion.129) | copy-start | bytes 3145732
  256.4 30.9 %copy-start.27 = (f32[512,512]{1,0:T(8,128)S(1)}, f32[512,512]{1,0:T(8,128)}, u32[]{:S(2)}) copy-start(f32[512,512]{1,0:T(8,128)} %copy-done.26) | copy-start | bytes 3145732
  257.6 32.7 %copy-start.31 = (f32[512,512]{1,0:T(8,128)}, f32[512,512]{1,0:T(8,128)S(1)}, u32[]{:S(2)}) copy-start(f32[512,512]{1,0:T(8,128)S(1)} %fusion.15) | copy-start | bytes 3145732
  283.9 6.4 %copy-start.22 = (f32[512,512]{1,0:T(8,128)S(1)}, f32[512,512]{1,0:T(8,128)}, u32[]{:S(2)}) copy-start(f32[512,512]{1,0:T(8,128)} %copy-done.21) | copy-start | bytes 3145732
  321.8 18.5 %copy-start.30 = (f32[512,512]{1,0:T(8,128)S(1)}, f32[512,512]{1,0:T(8,128)}, u32[]{:S(2)}) copy-start(f32[512,512]{1,0:T(8,128)} %fusion.6) | copy-start | bytes 3145732
  324.1 17.1 %copy-start.2 = (f32[4096,512]{1,0:T(8,128)S(1)}, f32[4096,512]{1,0:T(8,128)}, u32[]{:S(2)}) copy-start(f32[4096,512]{1,0:T(8,128)} %all-gather.35.cloned.1.call-done) | copy-start | bytes 25165828
  353.6 20.8 %copy-start.33 = (f32[1024,512]{1,0:T(8,128)S(1)}, f32[1024,512]{1,0:T(8,128)}, u32[]{:S(2)}) copy-start(f32[1024,512]{1,0:T(8,128)} %all-gather.37.cloned.1.call-done) | copy-start | bytes 6291460
  355.9 28.9 %copy-start.6 = (f32[2048,512]{1,0:T(8,128)S(1)}, f32[2048,512]{1,0:T(8,128)}, u32[]{:S(2)}) copy-start(f32[2048,512]{1,0:T(8,128)} %all-gather.39.cloned.1.call-done) | copy-start | bytes 12582916
  358.8 48.9 %copy-start.32 = (f32[512,512]{1,0:T(8,128)S(1)}, f32[512,512]{1,0:T(8,128)}, u32[]{:S(2)}) copy-start(f32[512,512]{1,0:T(8,128)} %copy-done.31) | copy-start | bytes 3145732
  416.5 18.3 %copy-start.24 = (f32[512,512]{1,0:T(8,128)S(1)}, f32[512,512]{1,0:T(8,128)}, u32[]{:S(2)}) copy-start(f32[512,512]{1,0:T(8,128)} %fusion.20) | copy-start | bytes 3145732
  418.8 17.0 %copy-start.1 = (f32[4096,512]{1,0:T(8,128)S(1)}, f32[4096,512]{1,0:T(8,128)}, u32[]{:S(2)}) copy-start(f32[4096,512]{1,0:T(8,128)} %all-gather.41.cloned.1.call-done) | copy-start | bytes 25165828
  (14 other events, 48.1 us)
Sparse Core Ops, SparseCore 0:
  9.8 36.9 all-gather.26
  48.6 33.3 all-gather.28
  83.8 16.8 all-gather.30
  102.3 17.1 all-gather.36
  121.2 51.1 all-gather.32
  174.1 51.0 all-gather.38
  227.0 94.7 all-gather.34
  323.6 92.9 all-gather.40
where the time goes:
time: 471 us; the launch traced here: 463 us
  waiting for transfers between devices  200 us (42%)
  matrix products  155 us (33%)
  blocking collectives  85 us (18%)
  between operations  15.1 us (3%)
  local copies, waits for them, and re-layouts  6.15 us (1%)
    all_gather x6, waiting for transfers between devices, prefix_by_axis(): pieces = jax.tree.map(lambda part: lax.all_gather(part, axis), so_far)  130 us
    dot_general x34, matrix products, chain_combine(): joined_map = jnp.dot(later[0], earlier[0], precision=highest)  74.4 us
    all_gather x6, blocking collectives, prefix_by_axis(): pieces = jax.tree.map(lambda part: lax.all_gather(part, axis), so_far)  68.3 us
    dot_general x34, matrix products, chain_combine(): joined_offset = jnp.dot(later[0], earlier[1], precision=highest) + later[1]  58.5 us
    all_gather x1, waiting for transfers between devices, shards(): lax.all_gather(filter_map, 'blk', axis=1, tiled=True)  38.1 us
    all_gather x1, waiting for transfers between devices, shards(): lax.all_gather(smoother_gain, 'blk', axis=1, tiled=True)  30.8 us
  transfers between devices with their start and end apart: 8, of which 8 were waited for; matrix products, arithmetic and copies ran while one was open for 25% of the time, Pallas kernels for 0%

commit v1 on v0

v1 whole, which is shorter than its diff:
```python
import functools

import jax
import jax.numpy as jnp
from jax import lax
from jax.experimental import pallas as pl
from jax.experimental.pallas import tpu as pltpu
from jax.sharding import Mesh
from jax.sharding import PartitionSpec as P

TM = ("tm_0", "tm_1", "tm_2")
MESH = pl.DeviceIdType.MESH
R = 128
B = 4
Z = 8
HIGHEST = lax.Precision.HIGHEST


def mat(a, b):
    return jnp.dot(a, b, precision=HIGHEST, preferred_element_type=jnp.float32)


def spread(row):
    return jnp.broadcast_to(row, (R, R)).T


def row_dot(pairs):
    total = None
    for a, u in pairs:
        total = a * u if total is None else total + a * u
    return jnp.sum(total.T, axis=0, keepdims=True)


def fold(product):
    return jnp.sum(product.reshape(R // 8, 8, R), axis=0)


def cut(block, k):
    return block[:, k * R : (k + 1) * R]


def kernel(
    prior,
    after,
    filter_map,
    smoother_gain,
    smoother_map,
    obs_gain,
    observations,
    filtered_out,
    smoothed_out,
    full,
    last,
    help_rows,
    pull_map,
    gain,
    tails,
    prefix,
    columns,
    spreads,
    shift_spread,
    shifts,
    stage,
    drives,
    offsets,
    entering,
    middle,
    leaving,
    rows_out,
    states,
    smoothed_in,
    seen,
    load_sem,
    send_sem,
    full_sem,
    last_sem,
    drive_sem,
    column_sem,
    shift_y_sem,
    shift_x_sem,
    hop_sem,
    state_sem,
    smoothed_sem,
    gate_sem,
):
    z, x, y = lax.axis_index("tm_0"), lax.axis_index("tm_1"), lax.axis_index("blk")
    core = lax.axis_index("tm_2")

    def branch(c):
        forward = c == 0
        own = filter_map if forward else smoother_gain
        other = smoother_gain if forward else filter_map
        place = x if forward else B - 1 - x
        level = z if forward else Z - 1 - z
        sends = []

        def x_at(p):
            return p if forward else B - 1 - p

        def turn(i, d):
            return lax.rem(i + d, B)

        def back(i, d):
            return lax.rem(i + B - d, B)

        def rows(i):
            return pl.ds(pl.multiple_of(i * R, R), R)

        def remote(src, dst, recv, device):
            return pltpu.make_async_remote_copy(
                src_ref=src,
                dst_ref=dst,
                send_sem=send_sem.at[len(sends)],
                recv_sem=recv,
                device_id=device,
                device_id_type=MESH,
            )

        def send(src, dst, recv, device):
            copy = remote(src, dst, recv, device)
            copy.start()
            sends.append(copy)

        def arrive(dst, recv, device):
            pltpu.make_async_remote_copy(
                src_ref=dst,
                dst_ref=dst,
                send_sem=send_sem.at[0],
                recv_sem=recv,
                device_id=device,
                device_id_type=MESH,
            ).wait_recv()

        loads = []

        def load(src, dst):
            copy = pltpu.make_async_copy(src, dst, load_sem.at[len(loads)])
            copy.start()
            loads.append(copy)

        load(own.at[c], full.at[0, rows(y)])
        load(own.at[1 - c], full.at[1, rows(y)])
        load(other.at[1 - c], help_rows.at[0])
        load(other.at[c], help_rows.at[1])
        load(obs_gain, gain)
        load(observations, seen)
        load(smoother_map, pull_map)

        barrier = pltpu.get_barrier_semaphore()
        peers = [(z, x, c, turn(y, d)) for d in (1, 2, 3)]
        peers += [(z, x, 1 - c, turn(y, d)) for d in (0, 1, 2, 3)]
        peers += [(z, turn(x, d), c, y) for d in (1, 2, 3)]
        peers += [(lax.rem(z + 1, Z), x, c, y), (lax.rem(z + Z - 1, Z), x, c, y)]
        for peer in peers:
            pl.semaphore_signal(barrier, inc=1, device_id=peer, device_id_type=MESH)
        pl.semaphore_wait(barrier, len(peers))

        def send_own():
            for n in (1, 0):
                loads[n].wait()
                for d in (1, 3, 2):
                    mine = full.at[n, rows(y)]
                    send(mine, mine, full_sem.at[n, d], (z, x, c, turn(y, d)))

        def send_help():
            loads[2].wait()
            for d in (0, 1, 3, 2):
                send(
                    help_rows.at[0],
                    full.at[2, rows(y)],
                    full_sem.at[2, d],
                    (z, x, 1 - c, turn(y, d)),
                )
            loads[3].wait()
            send(help_rows.at[1], last, last_sem, (z, x, 1 - c, y))

        def share_drives(to, first):
            if to == c:
                drives[y, first : first + 2] = stage[first : first + 2]
            for d in (1, 3, 2) if to == c else (0, 1, 3, 2):
                send(
                    stage.at[first : first + 2],
                    drives.at[y, first : first + 2],
                    drive_sem.at[c, d],
                    (z, x, to, turn(y, d)),
                )

        def await_drives():
            for cc in (c, 1 - c):
                first = 2 * cc if forward else 2 - 2 * cc
                for d in (1, 3, 2) if cc == c else (0, 1, 3, 2):
                    i = back(y, d)
                    arrive(
                        drives.at[i, first : first + 2], drive_sem.at[cc, d], (z, x, cc, i)
                    )

        def compose():
            for d in (0, 1, 3, 2):
                i = back(y, d)
                arrive(full.at[2, rows(i)], full_sem.at[2, d], (z, x, 1 - c, i))
            arrive(last, last_sem, (z, x, 1 - c, y))
            tails[0] = mat(last[...], full[2])
            for d in (1, 3, 2):
                i = back(y, d)
                arrive(full.at[1, rows(i)], full_sem.at[1, d], (z, x, c, i))
            tails[1] = mat(tails[0], full[1])
            for d in (1, 3, 2):
                i = back(y, d)
                arrive(full.at[0, rows(i)], full_sem.at[0, d], (z, x, c, i))
            whole = mat(tails[1], full[0])
            turned = [cut(whole, k).T for k in range(B)]
            for k in range(B):
                prefix[3, k] = turned[k]

            @pl.when(lax.rem(place, 2) == 0)
            def _():
                for k in range(B):
                    columns[place, y, k] = cut(whole, k)

            @pl.when(lax.rem(place, 2) == 1)
            def _():
                for k in range(B):
                    columns[place, y, k] = turned[k]

        def half(p, i, h):
            return columns.at[p, i, 2 * h : 2 * h + 2]

        def to_y(p, dp, h):
            for d in (1, 3, 2):
                mine = half(p, y, h)
                send(mine, mine, column_sem.at[dp, d, h], (z, x, c, turn(y, d)))

        def to_x(i, di, h):
            for d in (1, 3, 2):
                mine = half(place, i, h)
                send(mine, mine, column_sem.at[d, di, h], (z, x_at(turn(place, d)), c, y))

        def share_columns():
            to_y(place, 0, 0)
            to_x(y, 0, 1)
            to_y(place, 0, 1)
            to_x(y, 0, 0)

        def finish_prefixes():
            mine = full[1, rows(y)]
            tails[2] = mat(full[2, rows(y)], full[1])
            first = mat(mine, full[0])
            second = mat(tails[2], full[0])
            zeroth = full[0, rows(y)]
            for k in range(B):
                prefix[0, k] = cut(zeroth, k).T
                prefix[1, k] = cut(first, k).T
                prefix[2, k] = cut(second, k).T

        def forward_columns():
            for d in (1, 3, 2):
                i = back(y, d)
                arrive(half(place, i, 0), column_sem.at[0, d, 0], (z, x, c, i))
                to_x(i, d, 0)
                p = back(place, d)
                arrive(half(p, y, 1), column_sem.at[d, 0, 1], (z, x_at(p), c, y))
                to_y(p, d, 1)

        def await_columns():
            for d in (1, 3, 2):
                i = back(y, d)
                arrive(half(place, i, 1), column_sem.at[0, d, 1], (z, x, c, i))
                p = back(place, d)
                arrive(half(p, y, 0), column_sem.at[d, 0, 0], (z, x_at(p), c, y))
            for dp in (1, 3, 2):
                p = back(place, dp)
                for d in (1, 3, 2):
                    i = back(y, d)
                    arrive(half(p, i, 0), column_sem.at[dp, d, 0], (z, x_at(p), c, y))
                    arrive(half(p, i, 1), column_sem.at[dp, d, 1], (z, x, c, i))

        def column_offsets():
            def d(i):
                return [drives[k, i] for k in range(B)]

            def pairs(block, i):
                return [(cut(block, k), u) for k, u in enumerate(d(i))]

            last_shift = row_dot(pairs(tails[1], 0) + pairs(tails[0], 1) + pairs(last[...], 2))
            last_shift = last_shift + drives[y, 3]
            offsets[3] = last_shift
            shifts[place, y] = last_shift
            for e in (1, 3, 2):
                send(
                    shifts.at[place, y],
                    shifts.at[place, y],
                    shift_y_sem.at[e],
                    (z, x, c, turn(y, e)),
                )
            third = row_dot(pairs(tails[2], 0) + pairs(full[2, rows(y)], 1))
            offsets[2] = third + drives[y, 2]
            offsets[1] = row_dot(pairs(full[1, rows(y)], 0)) + drives[y, 1]
            offsets[0] = drives[y, 0]
            for e in (1, 3, 2):
                i = back(y, e)
                arrive(shifts.at[place, i], shift_y_sem.at[e], (z, x, c, i))
            for e in (1, 3, 2):
                send(
                    shifts.at[place],
                    shifts.at[place],
                    shift_x_sem.at[e],
                    (z, x_at(turn(place, e)), c, y),
                )

        def await_shifts():
            for e in (1, 3, 2):
                p = back(place, e)
                arrive(shifts.at[p], shift_x_sem.at[e], (z, x_at(p), c, y))
            for n in range(2):
                for k in range(B):
                    shift_spread[n, k] = spread(shifts[2 * n, k])

        def pair(n, state):
            for i in range(B):
                total = None
                for k in range(B):
                    term = columns[2 * n, i, k] * state[k]
                    total = term if total is None else total + term
                reduced = jnp.sum(total, axis=1, keepdims=True)
                spreads[2 * n + 1, i] = jnp.broadcast_to(reduced, (R, R)) + shift_spread[n, i]
            result = []
            for i in range(B):
                total = None
                for k in range(B):
                    term = fold(columns[2 * n + 1, i, k] * spreads[2 * n + 1, k])
                    total = term if total is None else total + term
                result.append(jnp.sum(total, axis=0, keepdims=True) + shifts[2 * n + 1, i])
            return result

        def chain(start):
            up, down = (z + 1, z - 1) if forward else (z - 1, z + 1)

            @pl.when(level == 0)
            def _():
                entering[...] = start[...]

            @pl.when(level > 0)
            def _():
                arrive(entering, hop_sem, (down, x, c, y))

            state = pair(0, [entering[k] for k in range(B)])
            for k in range(B):
                middle[k] = state[k]
            state = pair(1, state)
            for k in range(B):
                leaving[k] = state[k]
            hop = remote(leaving, entering, hop_sem, (up, x, c, y))

            @pl.when(level < Z - 1)
            def _():
                hop.start()

            @pl.when(place == 0)
            def _():
                for k in range(B):
                    spreads[0, k] = spread(entering[k])

            @pl.when(place == 2)
            def _():
                for k in range(B):
                    spreads[2, k] = spread(middle[k])

            for i in range(4):
                total = None
                for k in range(B):
                    term = fold(prefix[i, k] * spreads[place, k])
                    total = term if total is None else total + term
                rows_out[i] = jnp.sum(total, axis=0, keepdims=True) + offsets[i]

            @pl.when(level < Z - 1)
            def _():
                hop.wait_send()

            sends.append(None)

        def share_states():
            states[y] = rows_out[0:2]
            for d in (1, 3, 2):
                send(
                    rows_out.at[0:2], states.at[y], state_sem.at[d], (z, x, 0, turn(y, d))
                )
            for d in (0, 1, 3, 2):
                send(
                    rows_out.at[2:4], states.at[y], state_sem.at[d], (z, x, 1, turn(y, d))
                )

        def pull():
            for d in (1, 3, 2) if forward else (0, 1, 3, 2):
                i = back(y, d)
                arrive(states.at[i], state_sem.at[d], (z, x, 0, i))
            loads[6].wait()
            first = 2 - 2 * c
            for l in range(2):
                block = pull_map[l]
                stage[first + 1 - l] = row_dot(
                    [(cut(block, k), states[k, l]) for k in range(B)]
                )
            share_drives(1, first)
            for l in range(2):
                filtered_out[l : l + 1] = states[y, l]

        def drive():
            loads[4].wait()
            loads[5].wait()
            for l in range(2):
                stage[2 * c + l] = row_dot([(gain[l], seen[l : l + 1])])
            share_drives(0, 2 * c)

        if forward:
            send_own()
            drive()
            compose()
            share_columns()
            finish_prefixes()
            forward_columns()
            await_drives()
            column_offsets()
            await_columns()
            pl.semaphore_signal(gate_sem, inc=1, device_id=(z, x, 1, y), device_id_type=MESH)
            send_help()
            await_shifts()
            chain(prior)
            share_states()
            pull()
            arrive(smoothed_in, smoothed_sem, (z, x, 1, y))
            for l in range(2):
                smoothed_out[l : l + 1] = smoothed_in[1 - l]
        else:
            send_help()
            drive()
            pl.semaphore_wait(gate_sem, 1)
            send_own()
            compose()
            share_columns()
            finish_prefixes()
            forward_columns()
            pull()
            await_drives()
            column_offsets()
            await_columns()
            await_shifts()
            chain(after)
            send(rows_out.at[2:4], smoothed_in, smoothed_sem, (z, x, 0, y))
            for l in range(2):
                smoothed_out[l : l + 1] = rows_out[1 - l]
        for copy in sends:
            if copy is not None:
                copy.wait_send()

    @pl.when(core == 0)
    def _():
        branch(0)

    @pl.when(core == 1)
    def _():
        branch(1)


def shards(prior_mean, after_mean, filter_map, smoother_gain, smoother_map, obs_gain, observations):
    f32 = jnp.float32
    n = B * R
    vmem = pl.BlockSpec(memory_space=pltpu.VMEM)
    hbm = pl.BlockSpec(memory_space=pl.ANY)
    dma = pltpu.SemaphoreType.DMA
    shapes = [
        (3, n, n), (R, n), (2, R, n), (2, R, n), (2, R, R), (3, R, n),
        (4, B, R, R), (4, B, B, R, R), (4, B, R, R), (2, B, R, R),
        (4, B, 1, R), (4, 1, R), (B, 4, 1, R), (4, 1, R),
        (B, 1, R), (B, 1, R), (B, 1, R), (4, 1, R), (B, 2, 1, R), (2, 1, R), (2, R),
    ]
    return pl.pallas_call(
        kernel,
        out_shape=(jax.ShapeDtypeStruct((2, R), f32), jax.ShapeDtypeStruct((2, R), f32)),
        in_specs=[vmem, vmem, hbm, hbm, hbm, hbm, hbm],
        out_specs=(vmem, vmem),
        scratch_shapes=[pltpu.VMEM(shape, f32) for shape in shapes]
        + [
            dma((7,)), dma((80,)), dma((3, B)), dma, dma((2, B)), dma((B, B, 2)),
            dma((B,)), dma((B,)), dma, dma((B,)), dma, pltpu.SemaphoreType.REGULAR,
        ],
        compiler_params=pltpu.CompilerParams(
            collective_id=0, has_side_effects=True, vmem_limit_bytes=40 * 2**20
        ),
        name="smoother",
    )(
        prior_mean.reshape(B, 1, R),
        after_mean.reshape(B, 1, R),
        filter_map,
        smoother_gain,
        smoother_map,
        obs_gain,
        observations,
    )


def solution(mesh):
    torus = Mesh(mesh.devices.reshape(8, 4, 2, mesh.shape["blk"]), (*TM, "blk"))
    in_specs = (
        P(),
        P(),
        P(TM, "blk", None),
        P(TM, "blk", None),
        P(TM, "blk", None),
        P(TM, "blk", None),
        P(TM, None),
    )
    out_specs = (P(TM, "blk"), P(TM, "blk"))
    return jax.shard_map(
        shards, mesh=torus, in_specs=in_specs, out_specs=out_specs, check_vma=False
    )
```

time: 471 us -> 115 us (0.24); the launches traced: 463 us -> 115 us
  waiting for transfers between devices: 200 us -> 0 us
  matrix products: 155 us -> 0 us
  Pallas kernels: 0 us -> 108 us
  blocking collectives: 85 us -> 0 us
  between operations: 15.1 us -> 0.66 us
    all_gather x8 -> x0, waiting for transfers between devices: 199 us -> none  [the longest x6 130 us: prefix_by_axis(): pieces = jax.tree.map(lambda part: lax.all_gather(part, axis), so_far)]
    dot_general x82 -> x0, matrix products: 155 us -> none  [the longest x34 74.4 us: chain_combine(): joined_map = jnp.dot(later[0], earlier[0], precision=highest)]
    pallas_call x0 -> x1, Pallas kernels: none -> 108 us  [shards(): pl.pallas_call(kernel, out_shape=(jax.ShapeDtypeStruct((2, R), f32), jax....]
    all_gather x8 -> x0, blocking collectives: 85 us -> none  [the longest x6 68.3 us: prefix_by_axis(): pieces = jax.tree.map(lambda part: lax.all_gather(part, axis), so_far)]
  transfers between devices with their start and end apart: 8 -> 0, of which waited for: 8 -> 0; matrix products, arithmetic and copies ran while one was open for 25% -> 0% of each run, Pallas kernels for 0% -> 0%
where the time goes in v1:
time: 115 us
  Pallas kernels  108 us (94%)
  local copies, waits for them, and re-layouts  6.51 us (6%)
    pallas_call x1, Pallas kernels, shards(): pl.pallas_call(kernel, out_shape=(jax.ShapeDtypeStruct((2, R), f32), jax....  108 us
    unnamed x16, local copies, waits for them, and re-layouts  6.51 us

profile of v1, /device:TPU:1, one launch (start us, length us, event | category | flops | bytes accessed | tf_op | source)
XLA Modules:
  0.0 115.0 jit_solution(17815442353708022084)
XLA Ops:
  0.6 0.0 copy-start.4
  0.6 0.0 copy-start.6
  0.7 0.7 copy-done.4
  1.3 0.0 copy-done.6
  1.3 0.0 copy-start
  1.3 1.0 copy-done
  2.4 0.0 copy-start.1
  2.4 1.0 copy-done.1
  3.4 0.0 copy-start.2
  3.4 1.0 copy-done.2
  4.5 0.0 copy-start.3
  4.5 0.9 copy-done.3
  5.4 0.0 copy-start.5
  5.4 0.7 copy-done.5
  6.0 107.8 %smoother.1 = (f32[2,128]{1,0:T(2,128)S(1)}, f32[2,128]{1,0:T(2,128)S(1)}) custom-call(f32[4,1,128]{2,1,0:T(1,128)S(1)} %bitcast.2, f32[4,1,128]{2,1,0:T(1,128)S(1)} %bitcast.3, f32[2,128,512]{2,1,0:T(8,128)S(1)} %copy-done, f32[2,128,512]{2,1,0:T(8,128)S(1)} %copy-done.1, f32[2,128,512]{2,1,0:T(8,128)S(1)} %copy-done.2, f32[2,128,128]{2,1,0:T(8,128)S(1)} %copy-done.3, ...), custom_call_target="tpu_custom_call" | custom-call | tf_op jit(solution)/shard_map/smoother/pallas_call | solution.py:476
  113.9 0.6 copy.11
  114.4 0.6 copy.12
Async XLA Ops:
  0.6 0.7 copy-start.4
  0.6 0.7 copy-start.6
  1.3 1.0 copy-start
  2.4 1.0 copy-start.1
  3.4 1.0 copy-start.2
  4.5 0.9 copy-start.3
  5.4 0.7 copy-start.5

commit v2 on v1

--- a/solution.py
+++ b/solution.py
@@ -13,6 +13,10 @@
 R = 128
 B = 4
 Z = 8
+SIDES = (1, 3)
+YX, XY = (0, 2), (2, 4)
+YX_PART, XY_PART = {1: (0, 1), 3: (1, 2)}, {1: (2, 3), 3: (3, 4)}
+VMEM_LIMIT = 67_043_328
 HIGHEST = lax.Precision.HIGHEST
 
 
@@ -47,8 +51,7 @@
     smoother_map,
     obs_gain,
     observations,
-    filtered_out,
-    smoothed_out,
+    both_out,
     full,
     last,
     help_rows,
@@ -70,6 +73,7 @@
     states,
     smoothed_in,
     seen,
+    start,
     load_sem,
     send_sem,
     full_sem,
@@ -83,6 +87,7 @@
     smoothed_sem,
     gate_sem,
 ):
+    filtered_out, smoothed_out = both_out.at[0], both_out.at[1]
     z, x, y = lax.axis_index("tm_0"), lax.axis_index("tm_1"), lax.axis_index("blk")
     core = lax.axis_index("tm_2")
 
@@ -145,6 +150,7 @@
         load(obs_gain, gain)
         load(observations, seen)
         load(smoother_map, pull_map)
+        load(prior if forward else after, start)
 
         barrier = pltpu.get_barrier_semaphore()
         peers = [(z, x, c, turn(y, d)) for d in (1, 2, 3)]
@@ -155,24 +161,41 @@
             pl.semaphore_signal(barrier, inc=1, device_id=peer, device_id_type=MESH)
         pl.semaphore_wait(barrier, len(peers))
 
+        def block(n, i, h=None):
+            if h is None:
+                return full.at[n, rows(i)]
+            return full.at[n, pl.ds(pl.multiple_of(i * R + h * (R // 2), R // 2), R // 2)]
+
         def send_own():
             for n in (1, 0):
                 loads[n].wait()
-                for d in (1, 3, 2):
-                    mine = full.at[n, rows(y)]
-                    send(mine, mine, full_sem.at[n, d], (z, x, c, turn(y, d)))
+                for d in (1, 3):
+                    mine = block(n, y)
+                    send(mine, mine, full_sem.at[n, d, 0], (z, x, c, turn(y, d)))
 
         def send_help():
             loads[2].wait()
-            for d in (0, 1, 3, 2):
+            for d in (1, 3, 0):
                 send(
                     help_rows.at[0],
-                    full.at[2, rows(y)],
-                    full_sem.at[2, d],
+                    block(2, y),
+                    full_sem.at[2, d, 0],
                     (z, x, 1 - c, turn(y, d)),
                 )
             loads[3].wait()
             send(help_rows.at[1], last, last_sem, (z, x, 1 - c, y))
+
+        def pass_on(n):
+            for d, h in ((1, 0), (3, 1)):
+                i = back(y, d)
+                arrive(block(n, i), full_sem.at[n, d, 0], (z, x, c, i))
+                mine = block(n, i, h)
+                send(mine, mine, full_sem.at[n, 2, h], (z, x, c, turn(y, d)))
+
+        def await_far(n):
+            for h in (0, 1):
+                i = back(y, 2)
+                arrive(block(n, i, h), full_sem.at[n, 2, h], (z, x, c, i))
 
         def share_drives(to, first):
             if to == c:
@@ -195,18 +218,18 @@
                     )
 
         def compose():
-            for d in (0, 1, 3, 2):
-                i = back(y, d)
-                arrive(full.at[2, rows(i)], full_sem.at[2, d], (z, x, 1 - c, i))
+            for n in (2, 1, 0):
+                pass_on(n)
+            arrive(block(2, y), full_sem.at[2, 0, 0], (z, x, 1 - c, y))
             arrive(last, last_sem, (z, x, 1 - c, y))
+            await_far(2)
             tails[0] = mat(last[...], full[2])
-            for d in (1, 3, 2):
-                i = back(y, d)
-                arrive(full.at[1, rows(i)], full_sem.at[1, d], (z, x, c, i))
+            await_far(1)
             tails[1] = mat(tails[0], full[1])
-            for d in (1, 3, 2):
-                i = back(y, d)
-                arrive(full.at[0, rows(i)], full_sem.at[0, d], (z, x, c, i))
+            if forward:
+                await_drives()
+                share_shift()
+            await_far(0)
             whole = mat(tails[1], full[0])
             turned = [cut(whole, k).T for k in range(B)]
             for k in range(B):
@@ -222,24 +245,25 @@
                 for k in range(B):
                     columns[place, y, k] = turned[k]
 
-        def half(p, i, h):
-            return columns.at[p, i, 2 * h : 2 * h + 2]
-
-        def to_y(p, dp, h):
-            for d in (1, 3, 2):
-                mine = half(p, y, h)
-                send(mine, mine, column_sem.at[dp, d, h], (z, x, c, turn(y, d)))
-
-        def to_x(i, di, h):
-            for d in (1, 3, 2):
-                mine = half(place, i, h)
-                send(mine, mine, column_sem.at[d, di, h], (z, x_at(turn(place, d)), c, y))
+        def piece(dp, d, k):
+            return columns.at[back(place, dp), back(y, d), k[0] : k[1]]
+
+        def to_y(dp, d, k, e):
+            mine = piece(dp, d, k)
+            send(mine, mine, column_sem.at[dp, (d + e) % B, k[0]], (z, x, c, turn(y, e)))
+
+        def to_x(dp, d, k, e):
+            mine = piece(dp, d, k)
+            device = (z, x_at(turn(place, e)), c, y)
+            send(mine, mine, column_sem.at[(dp + e) % B, d, k[0]], device)
+
+        def got(dp, d, k):
+            arrive(piece(dp, d, k), column_sem.at[dp, d, k[0]], (z, x, c, back(y, 1)))
 
         def share_columns():
-            to_y(place, 0, 0)
-            to_x(y, 0, 1)
-            to_y(place, 0, 1)
-            to_x(y, 0, 0)
+            for to, k in ((to_y, YX), (to_x, XY), (to_x, YX), (to_y, XY)):
+                for e in SIDES:
+                    to(0, 0, k, e)
 
         def finish_prefixes():
             mine = full[1, rows(y)]
@@ -252,60 +276,66 @@
                 prefix[1, k] = cut(first, k).T
                 prefix[2, k] = cut(second, k).T
 
+        def relay(d):
+            for e in SIDES:
+                got(e, d, YX)
+                to_x(e, d, YX_PART[e], e)
+                got(d, e, XY)
+                to_y(d, e, XY_PART[e], e)
+
         def forward_columns():
+            for e in SIDES:
+                got(0, e, YX)
+                to_y(0, e, YX_PART[e], e)
+                got(e, 0, XY)
+                to_x(e, 0, XY_PART[e], e)
+            if forward:
+                spread_shift()
+            for d in SIDES:
+                for e in SIDES:
+                    to_x(0, d, YX, e)
+                    to_y(d, 0, XY, e)
+            relay(0)
+            for e in SIDES:
+                got(0, 2, YX_PART[e])
+                got(2, 0, XY_PART[e])
+            for e in SIDES:
+                to_x(0, 2, YX, e)
+                to_y(2, 0, XY, e)
             for d in (1, 3, 2):
-                i = back(y, d)
-                arrive(half(place, i, 0), column_sem.at[0, d, 0], (z, x, c, i))
-                to_x(i, d, 0)
-                p = back(place, d)
-                arrive(half(p, y, 1), column_sem.at[d, 0, 1], (z, x_at(p), c, y))
-                to_y(p, d, 1)
+                relay(d)
 
         def await_columns():
-            for d in (1, 3, 2):
-                i = back(y, d)
-                arrive(half(place, i, 1), column_sem.at[0, d, 1], (z, x, c, i))
-                p = back(place, d)
-                arrive(half(p, y, 0), column_sem.at[d, 0, 0], (z, x_at(p), c, y))
-            for dp in (1, 3, 2):
-                p = back(place, dp)
-                for d in (1, 3, 2):
-                    i = back(y, d)
-                    arrive(half(p, i, 0), column_sem.at[dp, d, 0], (z, x_at(p), c, y))
-                    arrive(half(p, i, 1), column_sem.at[dp, d, 1], (z, x, c, i))
-
-        def column_offsets():
-            def d(i):
-                return [drives[k, i] for k in range(B)]
-
-            def pairs(block, i):
-                return [(cut(block, k), u) for k, u in enumerate(d(i))]
-
-            last_shift = row_dot(pairs(tails[1], 0) + pairs(tails[0], 1) + pairs(last[...], 2))
-            last_shift = last_shift + drives[y, 3]
-            offsets[3] = last_shift
-            shifts[place, y] = last_shift
+            for d in range(B):
+                for e in SIDES:
+                    got(2, d, YX_PART[e])
+                    got(d, 2, XY_PART[e])
+
+        def pairs(rows_of_map, i):
+            return [(cut(rows_of_map, k), drives[k, i]) for k in range(B)]
+
+        def share_shift():
+            parts = pairs(tails[1], 0) + pairs(tails[0], 1) + pairs(last[...], 2)
+            shift = row_dot(parts) + drives[y, 3]
+            offsets[3] = shift
+            shifts[place, y] = shift
+            mine = shifts.at[place, y]
             for e in (1, 3, 2):
-                send(
-                    shifts.at[place, y],
-                    shifts.at[place, y],
-                    shift_y_sem.at[e],
-                    (z, x, c, turn(y, e)),
-                )
+                send(mine, mine, shift_y_sem.at[e], (z, x, c, turn(y, e)))
+
+        def spread_shift():
+            for e in (1, 3, 2):
+                i = back(y, e)
+                arrive(shifts.at[place, i], shift_y_sem.at[e], (z, x, c, i))
+            mine = shifts.at[place]
+            for e in (1, 3, 2):
+                send(mine, mine, shift_x_sem.at[e], (z, x_at(turn(place, e)), c, y))
+
+        def other_offsets():
             third = row_dot(pairs(tails[2], 0) + pairs(full[2, rows(y)], 1))
             offsets[2] = third + drives[y, 2]
             offsets[1] = row_dot(pairs(full[1, rows(y)], 0)) + drives[y, 1]
             offsets[0] = drives[y, 0]
-            for e in (1, 3, 2):
-                i = back(y, e)
-                arrive(shifts.at[place, i], shift_y_sem.at[e], (z, x, c, i))
-            for e in (1, 3, 2):
-                send(
-                    shifts.at[place],
-                    shifts.at[place],
-                    shift_x_sem.at[e],
-                    (z, x_at(turn(place, e)), c, y),
-                )
 
         def await_shifts():
             for e in (1, 3, 2):
@@ -332,7 +362,7 @@
                 result.append(jnp.sum(total, axis=0, keepdims=True) + shifts[2 * n + 1, i])
             return result
 
-        def chain(start):
+        def chain():
             up, down = (z + 1, z - 1) if forward else (z - 1, z + 1)
 
             @pl.when(level == 0)
@@ -418,13 +448,13 @@
             share_columns()
             finish_prefixes()
             forward_columns()
-            await_drives()
-            column_offsets()
-            await_columns()
             pl.semaphore_signal(gate_sem, inc=1, device_id=(z, x, 1, y), device_id_type=MESH)
             send_help()
+            other_offsets()
             await_shifts()
-            chain(prior)
+            await_columns()
+            loads[7].wait()
+            chain()
             share_states()
             pull()
             arrive(smoothed_in, smoothed_sem, (z, x, 1, y))
@@ -441,10 +471,13 @@
             forward_columns()
             pull()
             await_drives()
-            column_offsets()
+            share_shift()
+            spread_shift()
+            other_offsets()
+            await_shifts()
             await_columns()
-            await_shifts()
-            chain(after)
+            loads[7].wait()
+            chain()
             send(rows_out.at[2:4], smoothed_in, smoothed_sem, (z, x, 0, y))
             for l in range(2):
                 smoothed_out[l : l + 1] = rows_out[1 - l]
@@ -465,26 +498,26 @@
     f32 = jnp.float32
     n = B * R
     vmem = pl.BlockSpec(memory_space=pltpu.VMEM)
-    hbm = pl.BlockSpec(memory_space=pl.ANY)
+    hbm = pl.BlockSpec(memory_space=pltpu.HBM)
     dma = pltpu.SemaphoreType.DMA
     shapes = [
         (3, n, n), (R, n), (2, R, n), (2, R, n), (2, R, R), (3, R, n),
         (4, B, R, R), (4, B, B, R, R), (4, B, R, R), (2, B, R, R),
         (4, B, 1, R), (4, 1, R), (B, 4, 1, R), (4, 1, R),
-        (B, 1, R), (B, 1, R), (B, 1, R), (4, 1, R), (B, 2, 1, R), (2, 1, R), (2, R),
+        (B, 1, R), (B, 1, R), (B, 1, R), (4, 1, R), (B, 2, 1, R), (2, 1, R), (2, R), (B, 1, R),
     ]
-    return pl.pallas_call(
+    both = pl.pallas_call(
         kernel,
-        out_shape=(jax.ShapeDtypeStruct((2, R), f32), jax.ShapeDtypeStruct((2, R), f32)),
-        in_specs=[vmem, vmem, hbm, hbm, hbm, hbm, hbm],
-        out_specs=(vmem, vmem),
+        out_shape=jax.ShapeDtypeStruct((2, 2, R), f32),
+        in_specs=[hbm] * 7,
+        out_specs=vmem,
         scratch_shapes=[pltpu.VMEM(shape, f32) for shape in shapes]
         + [
-            dma((7,)), dma((80,)), dma((3, B)), dma, dma((2, B)), dma((B, B, 2)),
+            dma((8,)), dma((96,)), dma((3, B, 2)), dma, dma((2, B)), dma((B, B, 4)),
             dma((B,)), dma((B,)), dma, dma((B,)), dma, pltpu.SemaphoreType.REGULAR,
         ],
         compiler_params=pltpu.CompilerParams(
-            collective_id=0, has_side_effects=True, vmem_limit_bytes=40 * 2**20
+            collective_id=0, has_side_effects=True, vmem_limit_bytes=VMEM_LIMIT
         ),
         name="smoother",
     )(
@@ -496,6 +529,7 @@
         obs_gain,
         observations,
     )
+    return both[0], both[1]
 
 
 def solution(mesh):

time: 115 us -> 97.3 us (0.85)
  Pallas kernels: 108 us -> 95.3 us
  local copies, waits for them, and re-layouts: 6.51 us -> 1.24 us
    pallas_call x1, Pallas kernels: 108 us -> 95.3 us  [shards(): pl.pallas_call(kernel, out_shape=jax.ShapeDtypeStruct((2, 2, R), f32), in...]
    unnamed x16 -> x0, local copies, waits for them, and re-layouts: 6.51 us -> none
    squeeze x0 -> x1, local copies, waits for them, and re-layouts: none -> 1.24 us  [shards(): return (both[0], both[1])]
where the time goes in v2:
time: 97.3 us; the launch traced here: 97.2 us
  Pallas kernels  95.3 us (98%)
  local copies, waits for them, and re-layouts  1.24 us (1%)
    pallas_call x1, Pallas kernels, shards(): pl.pallas_call(kernel, out_shape=jax.ShapeDtypeStruct((2, 2, R), f32), in...  95.3 us

profile of v2, /device:TPU:1, one launch (start us, length us, event | category | flops | bytes accessed | tf_op | source)
XLA Modules:
  0.0 97.2 jit_solution(8007893002074704076)
XLA Ops:
  0.6 95.3 %smoother.1 = f32[2,2,128]{2,1,0:T(2,128)} custom-call(f32[4,1,128]{2,1,0:T(1,128)} %bitcast.6, f32[4,1,128]{2,1,0:T(1,128)} %bitcast.7, f32[2,128,512]{2,1,0:T(8,128)} %filter_map.1, f32[2,128,512]{2,1,0:T(8,128)} %smoother_gain.1, f32[2,128,512]{2,1,0:T(8,128)} %smoother_map.1, f32[2,128,128]{2,1,0:T(8,128)} %obs_gain.1, f32[2,128]{1,0:T(2,128)} %observations.1), custom_call_target="tpu_custom_call" | custom-call | tf_op jit(solution)/shard_map/smoother/pallas_call | solution.py:509
  96.0 1.2 %slice_bitcast_fusion = (f32[2,128]{1,0:T(2,128)}, f32[2,128]{1,0:T(2,128)}) fusion(f32[2,2,128]{2,1,0:T(2,128)} %smoother.1), kind=kLoop, calls=%fused_computation | loop fusion | bytes 4096 | tf_op jit(solution)/shard_map/squeeze | solution.py:532

commit v3 on v2

--- a/solution.py
+++ b/solution.py
@@ -13,15 +13,21 @@
 R = 128
 B = 4
 Z = 8
+GATE = 3
 SIDES = (1, 3)
 YX, XY = (0, 2), (2, 4)
 YX_PART, XY_PART = {1: (0, 1), 3: (1, 2)}, {1: (2, 3), 3: (3, 4)}
 VMEM_LIMIT = 67_043_328
-HIGHEST = lax.Precision.HIGHEST
 
 
 def mat(a, b):
-    return jnp.dot(a, b, precision=HIGHEST, preferred_element_type=jnp.float32)
+    high, low = [], []
+    for value in (a, b):
+        top = value.astype(jnp.bfloat16)
+        high.append(top)
+        low.append((value - top.astype(jnp.float32)).astype(jnp.bfloat16))
+    dot = functools.partial(jnp.dot, preferred_element_type=jnp.float32)
+    return dot(high[0], high[1]) + (dot(high[0], low[1]) + dot(low[0], high[1]))
 
 
 def spread(row):
@@ -74,6 +80,10 @@
     smoothed_in,
     seen,
     start,
+    back_tails,
+    pulled,
+    back_shift,
+    filtered_in,
     load_sem,
     send_sem,
     full_sem,
@@ -86,6 +96,12 @@
     state_sem,
     smoothed_sem,
     gate_sem,
+    pull_sem,
+    tails_sem,
+    pulled_sem,
+    drives_sem,
+    back_shift_sem,
+    filtered_sem,
 ):
     filtered_out, smoothed_out = both_out.at[0], both_out.at[1]
     z, x, y = lax.axis_index("tm_0"), lax.axis_index("tm_1"), lax.axis_index("blk")
@@ -149,14 +165,14 @@
         load(other.at[c], help_rows.at[1])
         load(obs_gain, gain)
         load(observations, seen)
-        load(smoother_map, pull_map)
+        load(smoother_map, pull_map.at[2 * c : 2 * c + 2])
         load(prior if forward else after, start)
 
         barrier = pltpu.get_barrier_semaphore()
         peers = [(z, x, c, turn(y, d)) for d in (1, 2, 3)]
-        peers += [(z, x, 1 - c, turn(y, d)) for d in (0, 1, 2, 3)]
         peers += [(z, turn(x, d), c, y) for d in (1, 2, 3)]
         peers += [(lax.rem(z + 1, Z), x, c, y), (lax.rem(z + Z - 1, Z), x, c, y)]
+        peers += [(z, turn(x, e), 1 - c, turn(y, d)) for e in range(B) for d in range(B)]
         for peer in peers:
             pl.semaphore_signal(barrier, inc=1, device_id=peer, device_id_type=MESH)
         pl.semaphore_wait(barrier, len(peers))
@@ -169,19 +185,15 @@
         def send_own():
             for n in (1, 0):
                 loads[n].wait()
-                for d in (1, 3):
+                for d in SIDES:
                     mine = block(n, y)
                     send(mine, mine, full_sem.at[n, d, 0], (z, x, c, turn(y, d)))
 
         def send_help():
             loads[2].wait()
             for d in (1, 3, 0):
-                send(
-                    help_rows.at[0],
-                    block(2, y),
-                    full_sem.at[2, d, 0],
-                    (z, x, 1 - c, turn(y, d)),
-                )
+                device = (z, x, 1 - c, turn(y, d))
+                send(help_rows.at[0], block(2, y), full_sem.at[2, d, 0], device)
             loads[3].wait()
             send(help_rows.at[1], last, last_sem, (z, x, 1 - c, y))
 
@@ -197,29 +209,31 @@
                 i = back(y, 2)
                 arrive(block(n, i, h), full_sem.at[n, 2, h], (z, x, c, i))
 
-        def share_drives(to, first):
-            if to == c:
-                drives[y, first : first + 2] = stage[first : first + 2]
-            for d in (1, 3, 2) if to == c else (0, 1, 3, 2):
-                send(
-                    stage.at[first : first + 2],
-                    drives.at[y, first : first + 2],
-                    drive_sem.at[c, d],
-                    (z, x, to, turn(y, d)),
-                )
+        def drive():
+            loads[4].wait()
+            loads[5].wait()
+            first = 2 * c
+            for l in range(2):
+                stage[first + l] = row_dot([(gain[l], seen[l : l + 1])])
+            mine = stage.at[first : first + 2]
+            if forward:
+                drives[y, 0:2] = stage[0:2]
+            for d in (1, 3, 2) if forward else (0, 1, 3, 2):
+                target = drives.at[y, first : first + 2]
+                send(mine, target, drive_sem.at[c, d], (z, x, 0, turn(y, d)))
 
         def await_drives():
-            for cc in (c, 1 - c):
-                first = 2 * cc if forward else 2 - 2 * cc
-                for d in (1, 3, 2) if cc == c else (0, 1, 3, 2):
+            for cc in (0, 1):
+                for d in (1, 3, 2) if cc == 0 else (0, 1, 3, 2):
                     i = back(y, d)
-                    arrive(
-                        drives.at[i, first : first + 2], drive_sem.at[cc, d], (z, x, cc, i)
-                    )
+                    target = drives.at[i, 2 * cc : 2 * cc + 2]
+                    arrive(target, drive_sem.at[cc, d], (z, x, cc, i))
 
         def compose():
             for n in (2, 1, 0):
                 pass_on(n)
+            if forward:
+                send_help()
             arrive(block(2, y), full_sem.at[2, 0, 0], (z, x, 1 - c, y))
             arrive(last, last_sem, (z, x, 1 - c, y))
             await_far(2)
@@ -266,10 +280,9 @@
                     to(0, 0, k, e)
 
         def finish_prefixes():
-            mine = full[1, rows(y)]
             tails[2] = mat(full[2, rows(y)], full[1])
-            first = mat(mine, full[0])
-            second = mat(tails[2], full[0])
+            both = mat(jnp.concatenate([full[1, rows(y)], tails[2]], axis=0), full[0])
+            first, second = both[:R], both[R:]
             zeroth = full[0, rows(y)]
             for k in range(B):
                 prefix[0, k] = cut(zeroth, k).T
@@ -295,21 +308,28 @@
                 for e in SIDES:
                     to_x(0, d, YX, e)
                     to_y(d, 0, XY, e)
+            if forward:
+                open_gate(2)
             relay(0)
             for e in SIDES:
                 got(0, 2, YX_PART[e])
                 got(2, 0, XY_PART[e])
-            for e in SIDES:
+            for e in (1, 3, 2):
                 to_x(0, 2, YX, e)
                 to_y(2, 0, XY, e)
-            for d in (1, 3, 2):
+            for d in (1, 3):
                 relay(d)
+            for e in SIDES:
+                got(e, 2, YX)
+                got(2, e, XY)
 
         def await_columns():
-            for d in range(B):
+            for d in (0, 1, 3):
                 for e in SIDES:
                     got(2, d, YX_PART[e])
                     got(d, 2, XY_PART[e])
+            got(2, 2, YX)
+            got(2, 2, XY)
 
         def pairs(rows_of_map, i):
             return [(cut(rows_of_map, k), drives[k, i]) for k in range(B)]
@@ -338,9 +358,16 @@
             offsets[0] = drives[y, 0]
 
         def await_shifts():
-            for e in (1, 3, 2):
-                p = back(place, e)
-                arrive(shifts.at[p], shift_x_sem.at[e], (z, x_at(p), c, y))
+            if forward:
+                for e in (1, 3, 2):
+                    p = back(place, e)
+                    arrive(shifts.at[p], shift_x_sem.at[e], (z, x_at(p), c, y))
+            else:
+                for e in range(B):
+                    p = back(place, e)
+                    for d in range(B):
+                        i = back(y, d)
+                        arrive(shifts.at[p, i], back_shift_sem.at[e, d], (z, x_at(p), 0, i))
             for n in range(2):
                 for k in range(B):
                     shift_spread[n, k] = spread(shifts[2 * n, k])
@@ -362,6 +389,17 @@
                 result.append(jnp.sum(total, axis=0, keepdims=True) + shifts[2 * n + 1, i])
             return result
 
+        def open_gate(n):
+            if n == GATE:
+                pl.semaphore_signal(
+                    gate_sem, inc=1, device_id=(z, x, 1, y), device_id_type=MESH
+                )
+
+        def back_offsets():
+            arrive(drives, drives_sem, (z, x, 0, y))
+            other_offsets()
+            offsets[3] = shifts[place, y]
+
         def chain():
             up, down = (z + 1, z - 1) if forward else (z - 1, z + 1)
 
@@ -371,6 +409,8 @@
 
             @pl.when(level > 0)
             def _():
+                if not forward:
+                    back_offsets()
                 arrive(entering, hop_sem, (down, x, c, y))
 
             state = pair(0, [entering[k] for k in range(B)])
@@ -395,6 +435,12 @@
                 for k in range(B):
                     spreads[2, k] = spread(middle[k])
 
+            if not forward:
+
+                @pl.when(level == 0)
+                def _():
+                    back_offsets()
+
             for i in range(4):
                 total = None
                 for k in range(B):
@@ -409,47 +455,47 @@
             sends.append(None)
 
         def share_states():
-            states[y] = rows_out[0:2]
+            states[y] = rows_out[...]
             for d in (1, 3, 2):
-                send(
-                    rows_out.at[0:2], states.at[y], state_sem.at[d], (z, x, 0, turn(y, d))
-                )
-            for d in (0, 1, 3, 2):
-                send(
-                    rows_out.at[2:4], states.at[y], state_sem.at[d], (z, x, 1, turn(y, d))
-                )
-
-        def pull():
-            for d in (1, 3, 2) if forward else (0, 1, 3, 2):
+                send(rows_out, states.at[y], state_sem.at[d], (z, x, 0, turn(y, d)))
+            send(rows_out.at[2:4], filtered_in, filtered_sem, (z, x, 1, y))
+            for d in (1, 3, 2):
                 i = back(y, d)
                 arrive(states.at[i], state_sem.at[d], (z, x, 0, i))
+
+        def pull():
             loads[6].wait()
-            first = 2 - 2 * c
-            for l in range(2):
-                block = pull_map[l]
-                stage[first + 1 - l] = row_dot(
-                    [(cut(block, k), states[k, l]) for k in range(B)]
-                )
-            share_drives(1, first)
-            for l in range(2):
-                filtered_out[l : l + 1] = states[y, l]
-
-        def drive():
-            loads[4].wait()
-            loads[5].wait()
-            for l in range(2):
-                stage[2 * c + l] = row_dot([(gain[l], seen[l : l + 1])])
-            share_drives(0, 2 * c)
+            arrive(pull_map.at[2:4], pull_sem, (z, x, 1, y))
+            for i in range(4):
+                step = pull_map[3 - i]
+                pulled[y, i] = row_dot([(cut(step, k), states[k, 3 - i]) for k in range(B)])
+            mine = pulled.at[y]
+            for d in (1, 3, 2):
+                send(mine, mine, pulled_sem.at[d], (z, x, 0, turn(y, d)))
+            arrive(back_tails, tails_sem, (z, x, 1, y))
+            for d in (1, 3, 2):
+                i = back(y, d)
+                arrive(pulled.at[i], pulled_sem.at[d], (z, x, 0, i))
+            maps = (back_tails[1], back_tails[0], help_rows[1])
+            parts = [(cut(a, k), pulled[k, i]) for i, a in enumerate(maps) for k in range(B)]
+            back_shift[...] = row_dot(parts) + pulled[y, 3]
+            p = B - 1 - x
+            for e in range(B):
+                for d in range(B):
+                    device = (z, B - 1 - turn(p, e), 1, turn(y, d))
+                    send(back_shift, shifts.at[p, y], back_shift_sem.at[e, d], device)
+            send(pulled, drives, drives_sem, (z, x, 1, y))
 
         if forward:
             send_own()
             drive()
             compose()
+            open_gate(0)
             share_columns()
+            open_gate(1)
             finish_prefixes()
             forward_columns()
-            pl.semaphore_signal(gate_sem, inc=1, device_id=(z, x, 1, y), device_id_type=MESH)
-            send_help()
+            open_gate(3)
             other_offsets()
             await_shifts()
             await_columns()
@@ -457,29 +503,31 @@
             chain()
             share_states()
             pull()
+            for l in range(2):
+                filtered_out[l : l + 1] = rows_out[l]
             arrive(smoothed_in, smoothed_sem, (z, x, 1, y))
             for l in range(2):
                 smoothed_out[l : l + 1] = smoothed_in[1 - l]
         else:
             send_help()
             drive()
+            loads[6].wait()
+            send(pull_map.at[2:4], pull_map.at[2:4], pull_sem, (z, x, 0, y))
             pl.semaphore_wait(gate_sem, 1)
             send_own()
             compose()
+            send(tails.at[0:2], back_tails, tails_sem, (z, x, 0, y))
             share_columns()
             finish_prefixes()
             forward_columns()
-            pull()
-            await_drives()
-            share_shift()
-            spread_shift()
-            other_offsets()
             await_shifts()
             await_columns()
             loads[7].wait()
             chain()
             send(rows_out.at[2:4], smoothed_in, smoothed_sem, (z, x, 0, y))
+            arrive(filtered_in, filtered_sem, (z, x, 0, y))
             for l in range(2):
+                filtered_out[l : l + 1] = filtered_in[l]
                 smoothed_out[l : l + 1] = rows_out[1 - l]
         for copy in sends:
             if copy is not None:
@@ -501,10 +549,11 @@
     hbm = pl.BlockSpec(memory_space=pltpu.HBM)
     dma = pltpu.SemaphoreType.DMA
     shapes = [
-        (3, n, n), (R, n), (2, R, n), (2, R, n), (2, R, R), (3, R, n),
+        (3, n, n), (R, n), (2, R, n), (4, R, n), (2, R, R), (3, R, n),
         (4, B, R, R), (4, B, B, R, R), (4, B, R, R), (2, B, R, R),
         (4, B, 1, R), (4, 1, R), (B, 4, 1, R), (4, 1, R),
-        (B, 1, R), (B, 1, R), (B, 1, R), (4, 1, R), (B, 2, 1, R), (2, 1, R), (2, R), (B, 1, R),
+        (B, 1, R), (B, 1, R), (B, 1, R), (4, 1, R), (B, 4, 1, R), (2, 1, R), (2, R), (B, 1, R),
+        (2, R, n), (B, 4, 1, R), (1, R), (2, 1, R),
     ]
     both = pl.pallas_call(
         kernel,
@@ -515,6 +564,7 @@
         + [
             dma((8,)), dma((96,)), dma((3, B, 2)), dma, dma((2, B)), dma((B, B, 4)),
             dma((B,)), dma((B,)), dma, dma((B,)), dma, pltpu.SemaphoreType.REGULAR,
+            dma, dma, dma((B,)), dma, dma((B, B)), dma,
         ],
         compiler_params=pltpu.CompilerParams(
             collective_id=0, has_side_effects=True, vmem_limit_bytes=VMEM_LIMIT

time: 97.3 us -> 96.5 us (level)
  no operation moved by 1% of the time
where the time goes in v3:
time: 96.5 us; the launch traced here: 96.4 us
  Pallas kernels  94.5 us (98%)
  local copies, waits for them, and re-layouts  1.24 us (1%)
    pallas_call x1, Pallas kernels, shards(): pl.pallas_call(kernel, out_shape=jax.ShapeDtypeStruct((2, 2, R), f32), in...  94.5 us

profile of v3, /device:TPU:1, one launch (start us, length us, event | category | flops | bytes accessed | tf_op | source)
XLA Modules:
  0.0 96.4 jit_solution(12272516695804782880)
XLA Ops:
  0.6 94.5 %smoother.1 = f32[2,2,128]{2,1,0:T(2,128)} custom-call(f32[4,1,128]{2,1,0:T(1,128)} %bitcast.6, f32[4,1,128]{2,1,0:T(1,128)} %bitcast.7, f32[2,128,512]{2,1,0:T(8,128)} %filter_map.1, f32[2,128,512]{2,1,0:T(8,128)} %smoother_gain.1, f32[2,128,512]{2,1,0:T(8,128)} %smoother_map.1, f32[2,128,128]{2,1,0:T(8,128)} %obs_gain.1, f32[2,128]{1,0:T(2,128)} %observations.1), custom_call_target="tpu_custom_call" | custom-call | tf_op jit(solution)/shard_map/smoother/pallas_call | solution.py:558
  95.2 1.2 %slice_bitcast_fusion = (f32[2,128]{1,0:T(2,128)}, f32[2,128]{1,0:T(2,128)}) fusion(f32[2,2,128]{2,1,0:T(2,128)} %smoother.1), kind=kLoop, calls=%fused_computation | loop fusion | bytes 4096 | tf_op jit(solution)/shard_map/squeeze | solution.py:582

commit v4 on v3

--- a/solution.py
+++ b/solution.py
@@ -13,7 +13,6 @@
 R = 128
 B = 4
 Z = 8
-GATE = 3
 SIDES = (1, 3)
 YX, XY = (0, 2), (2, 4)
 YX_PART, XY_PART = {1: (0, 1), 3: (1, 2)}, {1: (2, 3), 3: (3, 4)}
@@ -84,6 +83,7 @@
     pulled,
     back_shift,
     filtered_in,
+    first,
     load_sem,
     send_sem,
     full_sem,
@@ -93,7 +93,6 @@
     shift_y_sem,
     shift_x_sem,
     hop_sem,
-    state_sem,
     smoothed_sem,
     gate_sem,
     pull_sem,
@@ -245,10 +244,6 @@
                 share_shift()
             await_far(0)
             whole = mat(tails[1], full[0])
-            turned = [cut(whole, k).T for k in range(B)]
-            for k in range(B):
-                prefix[3, k] = turned[k]
-
             @pl.when(lax.rem(place, 2) == 0)
             def _():
                 for k in range(B):
@@ -257,7 +252,7 @@
             @pl.when(lax.rem(place, 2) == 1)
             def _():
                 for k in range(B):
-                    columns[place, y, k] = turned[k]
+                    columns[place, y, k] = cut(whole, k).T
 
         def piece(dp, d, k):
             return columns.at[back(place, dp), back(y, d), k[0] : k[1]]
@@ -280,6 +275,16 @@
                     to(0, 0, k, e)
 
         def finish_prefixes():
+            @pl.when(lax.rem(place, 2) == 0)
+            def _():
+                for k in range(B):
+                    prefix[3, k] = columns[place, y, k].T
+
+            @pl.when(lax.rem(place, 2) == 1)
+            def _():
+                for k in range(B):
+                    prefix[3, k] = columns[place, y, k]
+
             tails[2] = mat(full[2, rows(y)], full[1])
             both = mat(jnp.concatenate([full[1, rows(y)], tails[2]], axis=0), full[0])
             first, second = both[:R], both[R:]
@@ -308,8 +313,6 @@
                 for e in SIDES:
                     to_x(0, d, YX, e)
                     to_y(d, 0, XY, e)
-            if forward:
-                open_gate(2)
             relay(0)
             for e in SIDES:
                 got(0, 2, YX_PART[e])
@@ -337,7 +340,6 @@
         def share_shift():
             parts = pairs(tails[1], 0) + pairs(tails[0], 1) + pairs(last[...], 2)
             shift = row_dot(parts) + drives[y, 3]
-            offsets[3] = shift
             shifts[place, y] = shift
             mine = shifts.at[place, y]
             for e in (1, 3, 2):
@@ -389,11 +391,60 @@
                 result.append(jnp.sum(total, axis=0, keepdims=True) + shifts[2 * n + 1, i])
             return result
 
-        def open_gate(n):
-            if n == GATE:
-                pl.semaphore_signal(
-                    gate_sem, inc=1, device_id=(z, x, 1, y), device_id_type=MESH
-                )
+        def open_gate():
+            device = (z, x, 1, y)
+            pl.semaphore_signal(gate_sem, inc=1, device_id=device, device_id_type=MESH)
+
+        def expand():
+            def row_of(n, k):
+                return spreads[n, k].T[0:1]
+
+            ends = (
+                lambda k: entering[k],
+                lambda k: row_of(1, k),
+                lambda k: middle[k],
+                lambda k: row_of(3, k),
+                lambda k: leaving[k],
+            )
+            for n in range(B):
+
+                @pl.when(place == n)
+                def _():
+                    for k in range(B):
+                        first[k] = ends[n](k)
+                        states[k, 3] = ends[n + 1](k)
+
+            row = [first[k] for k in range(B)]
+            for i in range(3):
+                maps = [full[i, k * R : (k + 1) * R] for k in range(B)]
+                row = [
+                    row_dot([(cut(a, j), row[j]) for j in range(B)]) + drives[k, i]
+                    for k, a in enumerate(maps)
+                ]
+                for k in range(B):
+                    states[k, i] = row[k]
+
+        def column_rows():
+            @pl.when(place == 0)
+            def _():
+                for k in range(B):
+                    spreads[0, k] = spread(entering[k])
+
+            @pl.when(place == 2)
+            def _():
+                for k in range(B):
+                    spreads[2, k] = spread(middle[k])
+
+            @pl.when(level == 0)
+            def _():
+                back_offsets()
+
+            for i in range(4):
+                total = None
+                for k in range(B):
+                    term = fold(prefix[i, k] * spreads[place, k])
+                    total = term if total is None else total + term
+                rows_out[i] = jnp.sum(total, axis=0, keepdims=True) + offsets[i]
 
         def back_offsets():
             arrive(drives, drives_sem, (z, x, 0, y))
@@ -425,28 +476,10 @@
             def _():
                 hop.start()
 
-            @pl.when(place == 0)
-            def _():
-                for k in range(B):
-                    spreads[0, k] = spread(entering[k])
-
-            @pl.when(place == 2)
-            def _():
-                for k in range(B):
-                    spreads[2, k] = spread(middle[k])
-
-            if not forward:
-
-                @pl.when(level == 0)
-                def _():
-                    back_offsets()
-
-            for i in range(4):
-                total = None
-                for k in range(B):
-                    term = fold(prefix[i, k] * spreads[place, k])
-                    total = term if total is None else total + term
-                rows_out[i] = jnp.sum(total, axis=0, keepdims=True) + offsets[i]
+            if forward:
+                expand()
+            else:
+                column_rows()
 
             @pl.when(level < Z - 1)
             def _():
@@ -455,13 +488,9 @@
             sends.append(None)
 
         def share_states():
-            states[y] = rows_out[...]
-            for d in (1, 3, 2):
-                send(rows_out, states.at[y], state_sem.at[d], (z, x, 0, turn(y, d)))
-            send(rows_out.at[2:4], filtered_in, filtered_sem, (z, x, 1, y))
-            for d in (1, 3, 2):
-                i = back(y, d)
-                arrive(states.at[i], state_sem.at[d], (z, x, 0, i))
+            send(states.at[y, 2:4], filtered_in, filtered_sem, (z, x, 1, y))
+            for l in range(2):
+                filtered_out[l : l + 1] = states[y, l]
 
         def pull():
             loads[6].wait()
@@ -490,21 +519,15 @@
             send_own()
             drive()
             compose()
-            open_gate(0)
             share_columns()
-            open_gate(1)
-            finish_prefixes()
             forward_columns()
-            open_gate(3)
-            other_offsets()
+            open_gate()
             await_shifts()
             await_columns()
             loads[7].wait()
             chain()
+            pull()
             share_states()
-            pull()
-            for l in range(2):
-                filtered_out[l : l + 1] = rows_out[l]
             arrive(smoothed_in, smoothed_sem, (z, x, 1, y))
             for l in range(2):
                 smoothed_out[l : l + 1] = smoothed_in[1 - l]
@@ -553,7 +576,7 @@
         (4, B, R, R), (4, B, B, R, R), (4, B, R, R), (2, B, R, R),
         (4, B, 1, R), (4, 1, R), (B, 4, 1, R), (4, 1, R),
         (B, 1, R), (B, 1, R), (B, 1, R), (4, 1, R), (B, 4, 1, R), (2, 1, R), (2, R), (B, 1, R),
-        (2, R, n), (B, 4, 1, R), (1, R), (2, 1, R),
+        (2, R, n), (B, 4, 1, R), (1, R), (2, 1, R), (B, 1, R),
     ]
     both = pl.pallas_call(
         kernel,
@@ -563,7 +586,7 @@
         scratch_shapes=[pltpu.VMEM(shape, f32) for shape in shapes]
         + [
             dma((8,)), dma((96,)), dma((3, B, 2)), dma, dma((2, B)), dma((B, B, 4)),
-            dma((B,)), dma((B,)), dma, dma((B,)), dma, pltpu.SemaphoreType.REGULAR,
+            dma((B,)), dma((B,)), dma, dma, pltpu.SemaphoreType.REGULAR,
             dma, dma, dma((B,)), dma, dma((B, B)), dma,
         ],
         compiler_params=pltpu.CompilerParams(

time: 96.5 us -> 93 us (0.964)
  Pallas kernels: 94.5 us -> 91 us
    pallas_call x1, Pallas kernels: 94.5 us -> 91 us  [shards(): pl.pallas_call(kernel, out_shape=jax.ShapeDtypeStruct((2, 2, R), f32), in...]
where the time goes in v4:
time: 93 us; the launch traced here: 92.9 us
  Pallas kernels  91 us (98%)
  local copies, waits for them, and re-layouts  1.24 us (1%)
    pallas_call x1, Pallas kernels, shards(): pl.pallas_call(kernel, out_shape=jax.ShapeDtypeStruct((2, 2, R), f32), in...  91 us

profile of v4, /device:TPU:1, one launch (start us, length us, event | category | flops | bytes accessed | tf_op | source)
XLA Modules:
  0.0 92.9 jit_solution(15388121729239223008)
XLA Ops:
  0.6 91.0 %smoother.1 = f32[2,2,128]{2,1,0:T(2,128)} custom-call(f32[4,1,128]{2,1,0:T(1,128)} %bitcast.6, f32[4,1,128]{2,1,0:T(1,128)} %bitcast.7, f32[2,128,512]{2,1,0:T(8,128)} %filter_map.1, f32[2,128,512]{2,1,0:T(8,128)} %smoother_gain.1, f32[2,128,512]{2,1,0:T(8,128)} %smoother_map.1, f32[2,128,128]{2,1,0:T(8,128)} %obs_gain.1, f32[2,128]{1,0:T(2,128)} %observations.1), custom_call_target="tpu_custom_call" | custom-call | tf_op jit(solution)/shard_map/smoother/pallas_call | solution.py:581
  91.7 1.2 %slice_bitcast_fusion = (f32[2,128]{1,0:T(2,128)}, f32[2,128]{1,0:T(2,128)}) fusion(f32[2,2,128]{2,1,0:T(2,128)} %smoother.1), kind=kLoop, calls=%fused_computation | loop fusion | bytes 4096 | tf_op jit(solution)/shard_map/squeeze | solution.py:605

commit v5 on v4

--- a/solution.py
+++ b/solution.py
@@ -15,6 +15,7 @@
 Z = 8
 SIDES = (1, 3)
 YX, XY = (0, 2), (2, 4)
+FAR = sorted(((e, d) for e in range(B) for d in range(B)), key=lambda o: sum(min(i, B - i) for i in o))
 YX_PART, XY_PART = {1: (0, 1), 3: (1, 2)}, {1: (2, 3), 3: (3, 4)}
 VMEM_LIMIT = 67_043_328
 
@@ -364,15 +365,17 @@
                 for e in (1, 3, 2):
                     p = back(place, e)
                     arrive(shifts.at[p], shift_x_sem.at[e], (z, x_at(p), c, y))
+                for n in range(2):
+                    for k in range(B):
+                        shift_spread[n, k] = spread(shifts[2 * n, k])
             else:
-                for e in range(B):
-                    p = back(place, e)
-                    for d in range(B):
-                        i = back(y, d)
-                        arrive(shifts.at[p, i], back_shift_sem.at[e, d], (z, x_at(p), 0, i))
-            for n in range(2):
-                for k in range(B):
-                    shift_spread[n, k] = spread(shifts[2 * n, k])
+                for e, d in FAR:
+                    p, i = back(place, e), back(y, d)
+                    arrive(shifts.at[p, i], back_shift_sem.at[e, d], (z, x_at(p), 0, i))
+
+                    @pl.when(lax.rem(p, 2) == 0)
+                    def _():
+                        shift_spread[lax.div(p, 2), i] = spread(shifts[p, i])
 
         def pair(n, state):
             for i in range(B):
@@ -499,7 +502,7 @@
                 step = pull_map[3 - i]
                 pulled[y, i] = row_dot([(cut(step, k), states[k, 3 - i]) for k in range(B)])
             mine = pulled.at[y]
-            for d in (1, 3, 2):
+            for d in (2, 1, 3):
                 send(mine, mine, pulled_sem.at[d], (z, x, 0, turn(y, d)))
             arrive(back_tails, tails_sem, (z, x, 1, y))
             for d in (1, 3, 2):
@@ -509,10 +512,9 @@
             parts = [(cut(a, k), pulled[k, i]) for i, a in enumerate(maps) for k in range(B)]
             back_shift[...] = row_dot(parts) + pulled[y, 3]
             p = B - 1 - x
-            for e in range(B):
-                for d in range(B):
-                    device = (z, B - 1 - turn(p, e), 1, turn(y, d))
-                    send(back_shift, shifts.at[p, y], back_shift_sem.at[e, d], device)
+            for e, d in FAR[::-1]:
+                device = (z, B - 1 - turn(p, e), 1, turn(y, d))
+                send(back_shift, shifts.at[p, y], back_shift_sem.at[e, d], device)
             send(pulled, drives, drives_sem, (z, x, 1, y))
 
         if forward:
@@ -521,9 +523,9 @@
             compose()
             share_columns()
             forward_columns()
-            open_gate()
             await_shifts()
             await_columns()
+            open_gate()
             loads[7].wait()
             chain()
             pull()
@@ -539,10 +541,10 @@
             pl.semaphore_wait(gate_sem, 1)
             send_own()
             compose()
+            share_columns()
             send(tails.at[0:2], back_tails, tails_sem, (z, x, 0, y))
-            share_columns()
+            forward_columns()
             finish_prefixes()
-            forward_columns()
             await_shifts()
             await_columns()
             loads[7].wait()

time: 93 us -> 92.1 us (level)
    pallas_call x1, Pallas kernels: 91 us -> 90.1 us  [shards(): pl.pallas_call(kernel, out_shape=jax.ShapeDtypeStruct((2, 2, R), f32), in...]
where the time goes in v5:
time: 92.1 us; the launch traced here: 92 us
  Pallas kernels  90.1 us (98%)
  local copies, waits for them, and re-layouts  1.24 us (1%)
    pallas_call x1, Pallas kernels, shards(): pl.pallas_call(kernel, out_shape=jax.ShapeDtypeStruct((2, 2, R), f32), in...  90.1 us

profile of v5, /device:TPU:1, one launch (start us, length us, event | category | flops | bytes accessed | tf_op | source)
XLA Modules:
  0.0 92.0 jit_solution(6224949862319103459)
XLA Ops:
  0.6 90.1 %smoother.1 = f32[2,2,128]{2,1,0:T(2,128)} custom-call(f32[4,1,128]{2,1,0:T(1,128)} %bitcast.6, f32[4,1,128]{2,1,0:T(1,128)} %bitcast.7, f32[2,128,512]{2,1,0:T(8,128)} %filter_map.1, f32[2,128,512]{2,1,0:T(8,128)} %smoother_gain.1, f32[2,128,512]{2,1,0:T(8,128)} %smoother_map.1, f32[2,128,128]{2,1,0:T(8,128)} %obs_gain.1, f32[2,128]{1,0:T(2,128)} %observations.1), custom_call_target="tpu_custom_call" | custom-call | tf_op jit(solution)/shard_map/smoother/pallas_call | solution.py:583
  90.7 1.2 %slice_bitcast_fusion = (f32[2,128]{1,0:T(2,128)}, f32[2,128]{1,0:T(2,128)}) fusion(f32[2,2,128]{2,1,0:T(2,128)} %smoother.1), kind=kLoop, calls=%fused_computation | loop fusion | bytes 4096 | tf_op jit(solution)/shard_map/squeeze | solution.py:607
